TPU v7x, 32 devices: a whole 2x2x4 slice. The times are simulated.
32 devices in a mesh: dp: 8 (over z, x), rep: 4 (over y, core).
Axes of the slice: x: 2, y: 2, z: 4, core: 2. Of those that a mesh axis runs over, the one named last changes fastest.
Arguments:
- features: bfloat16 [5120, 8192], P('dp', 'rep'), may hold values from -6 to 6
- out_grads: bfloat16 [5120, 1024], P('dp'), may hold values from -12 to 12, as said below
- cold_sums: bfloat16 [8, 8192, 1024], P('dp', 'rep'), may hold values from -96 to 96
- weight: float32 [8192, 1024], P(('rep', 'dp')), may hold values from -3 to 3
- moment: float32 [8192, 1024], P(('rep', 'dp')), may hold values from -6 to 6
- second: float32 [8192, 1024], P(('rep', 'dp')), may hold values from 0.01 to 4
- ranks: int32 [8], replicated, may hold values from 0 to 7, each once
Outputs:
- new_weight: float32 [8192, 1024], P(('rep', 'dp'))
- new_moment: float32 [8192, 1024], P(('rep', 'dp'))
- new_second: float32 [8192, 1024], P(('rep', 'dp'))
- new_cold: bfloat16 [8, 8192, 1024], P('dp', 'rep')
- column_sq: float32 [1024], replicated
Inputs may be any that keep to these rules, and one draw needn't show every extreme that they name: `ranks`: each block number appears once. `out_grads`: column scales differ from column to column.
All inputs are finite; a program needn't handle non-finite values.
Results may differ from a plain program's by a relative error of at most 0.001.
Values sent between devices are 32-bit elements; how exact they have to be, the bound alone decides.
No kernel may reach another device: no remote copies, remote signals or barrier semaphores. Data moves between devices by JAX's collectives and lax.ppermute only.
A program may use at most 128 MiB of HBM per device.

v0:
```python
import jax
import jax.numpy as jnp
from jax import lax
from jax.sharding import PartitionSpec as P


def cycle(count):
    return list(range(1, count, 2)) + list(reversed(range(0, count, 2)))


def body(features, out_grads, cold_sums, weight, moment, second, ranks):
    blocks = ranks.shape[0]
    hot_count = blocks // 2
    width = out_grads.shape[1]
    local_rows = features.shape[1]
    grad = lax.dot_general(
        features, out_grads, (((0,), (0,)), ((), ())), preferred_element_type=jnp.float32
    )
    local = cold_sums[0].astype(jnp.float32) + grad
    hot_block = ranks < hot_count
    hot_col = jnp.repeat(hot_block, 128)
    new_cold = jnp.where(hot_col[None, :], jnp.float32(0.0), local).astype(jnp.bfloat16)[None]
    partial_sq = jnp.sum(local * local, axis=0)
    column_sq = lax.psum(partial_sq, ("dp", "rep"))
    picker = (ranks[None, :] == jnp.arange(hot_count, dtype=jnp.int32)[:, None]).astype(jnp.float32)
    packed = jnp.einsum(
        "rbk,sb->rsk",
        local.reshape(local_rows, blocks, 128),
        picker,
        precision=lax.Precision.HIGHEST,
    )
    members = cycle(lax.axis_size("dp"))
    part = packed.reshape(len(members), local_rows // len(members), hot_count * 128)
    ordered = jnp.concatenate([part[m] for m in members], axis=0)
    owned = lax.psum_scatter(
        ordered, "dp", scatter_dimension=0, tiled=True, axis_index_groups=[members]
    )
    owned_rows = owned.shape[0]
    spread = jnp.einsum(
        "rsk,sb->rbk",
        owned.reshape(owned_rows, hot_count, 128),
        picker,
        precision=lax.Precision.HIGHEST,
    )
    summed = spread.reshape(owned_rows, width)
    dp_count = lax.axis_size("dp")
    total_rows = local_rows * lax.axis_size("rep")
    rms = jnp.sqrt(column_sq / jnp.float32(total_rows * dp_count * features.shape[0]))
    clip = 1.0 / jnp.maximum(jnp.float32(1.0), rms)
    grad_mean = summed * clip[None, :] / jnp.float32(dp_count)
    moved = 0.9 * moment + 0.1 * grad_mean
    squared = 0.95 * second + 0.05 * grad_mean * grad_mean
    step_size = 0.05 * (moved / (1.0 - 0.9**10)) / (jnp.sqrt(squared / (1.0 - 0.95**10)) + 1e-08)
    new_moment = jnp.where(hot_col[None, :], moved, moment)
    new_second = jnp.where(hot_col[None, :], squared, second)
    new_weight = jnp.where(hot_col[None, :], weight - step_size, weight)
    return (new_weight, new_moment, new_second, new_cold, column_sq)


def solution(mesh):
    placed = (
        P("dp", "rep"),
        P("dp", None),
        P("dp", "rep", None),
        P(("rep", "dp"), None),
        P(("rep", "dp"), None),
        P(("rep", "dp"), None),
        P(),
    )
    return jax.shard_map(
        body,
        mesh=mesh,
        in_specs=placed,
        out_specs=(
            P(("rep", "dp"), None),
            P(("rep", "dp"), None),
            P(("rep", "dp"), None),
            P("dp", "rep", None),
            P(),
        ),
        check_vma=False,
    )
```

profile of v0, /device:TPU:0, one launch (start us, length us, event | category | flops | bytes accessed | tf_op | source)
XLA Modules:
  0.0 115.6 jit_solution(7516741653848244742)
XLA Ops:
  7.2 0.0 copy-start
  7.2 0.0 reduce-scatter.2.cloned.1.call-start
  7.2 6.6 %copy.12 = bf16[1,2048,1024]{1,2,0:T(8,128)(2,1)} copy(bf16[1,2048,1024]{2,1,0:T(8,128)(2,1)} %param.9) | data formatting | bytes 8388608 | tf_op args[2]
  13.8 0.0 copy-done
  13.8 8.2 %multiply_reduce_fusion = (f32[1024]{0:T(1024)S(1)}, f32[2048,1024]{0,1:T(8,128)}) fusion(bf16[640,2048]{1,0:T(8,128)(2,1)S(1)} %copy-done, bf16[640,1024]{1,0:T(8,128)(2,1)} %param.8, bf16[1,2048,1024]{1,2,0:T(8,128)(2,1)} %copy.12), kind=kOutput, calls=%fused_computation.2 | convolution fusion | flops 2692742144 | bytes 16519168 | tf_op jit(solution)/shard_map/dot_general | solution.py:16
  22.0 0.0 copy-start.2
  22.0 9.3 %copy.13 = f32[2048,8,128]{2,1,0:T(8,128)} copy(f32[2048,8,128]{0,2,1:T(8,128)} %bitcast.58) | data formatting | bytes 16777216 | tf_op jit(solution)/shard_map/reshape | solution.py:28
  31.3 0.0 copy-done.2
  31.3 7.4 %convolution_bitcast_fusion = f32[2048,4,128]{2,1,0:T(4,128)S(1)} fusion(f32[2048,8,128]{2,1,0:T(8,128)} %copy.13, s32[8]{0:T(128)S(1)} %copy-done.2), kind=kOutput, calls=%fused_computation.4 | convolution fusion | flops 100663328 | bytes 12582944 | tf_op jit(solution)/shard_map/rbk,sb->rsk/dot_general | solution.py:26
  38.7 0.3 fusion.9
  39.0 0.9 bitcast_dynamic-update-slice_fusion.7
  39.8 0.9 bitcast_dynamic-update-slice_fusion.6
  40.7 0.8 bitcast_dynamic-update-slice_fusion.5
  41.6 0.8 bitcast_dynamic-update-slice_fusion.4
  42.4 0.9 bitcast_dynamic-update-slice_fusion.3
  43.3 0.8 bitcast_dynamic-update-slice_fusion.2
  44.1 0.8 bitcast_dynamic-update-slice_fusion.1
  44.9 0.8 bitcast_dynamic-update-slice_fusion
  45.8 0.0 reduce-scatter.2.cloned.1.call-update
  45.8 0.1 broadcast_bitcast_fusion
  45.9 5.9 %fusion = bf16[1,2048,1024]{1,2,0:T(8,128)(2,1)} fusion(f32[2048,1024]{0,1:T(8,128)} %get-tuple-element.22, pred[1024]{0:T(1024)(128)(4,1)S(1)} %broadcast_bitcast_fusion), kind=kLoop, calls=%fused_computation.3 | loop fusion | flops 2097152 | bytes 12583936 | tf_op jit(solution)/shard_map/broadcast_in_dim | solution.py:22
  51.8 6.3 %copy.14 = bf16[1,2048,1024]{2,1,0:T(8,128)(2,1)} copy(bf16[1,2048,1024]{1,2,0:T(8,128)(2,1)} %fusion) | data formatting | bytes 8388608
  58.1 44.1 %psum.7 = f32[1024]{0:T(1024)S(1)} all-reduce(f32[1024]{0:T(1024)S(1)} %get-tuple-element.21), channel_id=1, replica_groups=mesh['dp'=8,'rep'=4] {'dp','rep'}, use_global_device_ids=true, to_apply=%region_2.3 | all-reduce | flops 1024 | bytes 8192 | tf_op jit(solution)/shard_map/psum | solution.py:24
  102.1 0.0 copy-start.1
  102.1 0.0 reduce-scatter.2.cloned.1.call-done
  102.1 1.2 %reshape.42 = f32[256,4,128]{2,1,0:T(4,128)S(1)} reshape(f32[256,512]{1,0:T(8,128)} %reduce-scatter.2.cloned.1.call-done) | data formatting | bytes 1048576 | tf_op jit(solution)/shard_map/reshape | solution.py:41
  103.4 0.7 fusion.4
  104.1 4.6 %fusion.2 = (f32[256,1024]{1,0:T(8,128)}, f32[256,1024]{1,0:T(8,128)}, f32[256,1024]{1,0:T(8,128)}) fusion(f32[256,1024]{1,0:T(8,128)} %param.12, f32[32,8,8,128]{3,2,1,0:T(8,128)S(1)} %bitcast.59, f32[1024]{0:T(1024)S(1)} %maximum_divide_fusion, pred[1024]{0:T(1024)(128)(4,1)S(1)} %broadcast_bitcast_fusion, f32[256,1024]{1,0:T(8,128)} %param.10, ...), kind=kLoop, calls=%fused_computation.10 | loop fusion | flops 4456448 | bytes 7345152 | tf_op jit(solution)/shard_map/jit(_where)/select_n | solution.py:55
  108.7 0.0 copy-done.1
  (2 shorter events, 0.0 us)
Async XLA Ops:
  7.2 6.6 %copy-start = (bf16[640,2048]{1,0:T(8,128)(2,1)S(1)}, bf16[640,2048]{1,0:T(8,128)(2,1)}, u32[]{:S(2)}) copy-start(bf16[640,2048]{1,0:T(8,128)(2,1)} %param.7) | copy-start | bytes 7864324
  7.2 95.0 %reduce-scatter.2.cloned.1.call-start = ((), (), s32[]{:S(2)}) async-start(), calls=%async_computation.1 | async-start | bytes 4718592 | tf_op jit(solution)/shard_map/reduce_scatter | solution.py:35
  22.0 9.3 %copy-start.2 = (s32[8]{0:T(128)S(1)}, s32[8]{0:T(128)}, u32[]{:S(2)}) copy-start(s32[8]{0:T(128)} %param.13) | copy-start | bytes 100
  102.1 6.6 %copy-start.1 = (f32[1024]{0:T(1024)}, f32[1024]{0:T(1024)S(1)}, u32[]{:S(2)}) copy-start(f32[1024]{0:T(1024)S(1)} %psum.7) | copy-start | bytes 12292
Sparse Core Ops, SparseCore 0:
  45.9 52.1 reduce-scatter.1
where the time goes:
time: 116 us
  blocking collectives  44.1 us (38%)
  local copies, waits for them, and re-layouts  30.5 us (26%)
  matrix products  16.3 us (14%)
  between operations  14.1 us (12%)
  other arithmetic  10.5 us (9%)
    psum x1, blocking collectives, body(): column_sq = lax.psum(partial_sq, ('dp', 'rep'))  44.1 us
    unnamed x15, local copies, waits for them, and re-layouts  18.8 us
    reshape x1, local copies, waits for them, and re-layouts, body(): local.reshape(local_rows, blocks, 128)  9.29 us
    dot_general x1, matrix products, body(): lax.dot_general(features, out_grads, (((0,), (0,)), ((), ())), preferred_...  8.15 us
    dot_general x1, matrix products, body(): jnp.einsum('rbk,sb->rsk', local.reshape(local_rows, blocks, 128), picker,...  7.42 us
    broadcast_in_dim x1, other arithmetic, body(): jnp.where(hot_col[None, :], jnp.float32(0.0), local).astype(jnp.bfloat16)  5.87 us
    select_n x1, other arithmetic, body(): new_second = jnp.where(hot_col[None, :], squared, second)  4.64 us
  transfers between devices with their start and end apart: 1, of which 0 were waited for; matrix products, arithmetic and copies ran while one was open for 11% of the time, Pallas kernels for 0%

commit v1 on v0

--- a/solution.py
+++ b/solution.py
@@ -21,7 +21,9 @@
     hot_col = jnp.repeat(hot_block, 128)
     new_cold = jnp.where(hot_col[None, :], jnp.float32(0.0), local).astype(jnp.bfloat16)[None]
     partial_sq = jnp.sum(local * local, axis=0)
-    column_sq = lax.psum(partial_sq, ("dp", "rep"))
+    column_sq = partial_sq
+    for pp in ("rep", "dp"):
+        column_sq = jax.lax.psum(column_sq, axis_name=pp)
     picker = (ranks[None, :] == jnp.arange(hot_count, dtype=jnp.int32)[:, None]).astype(jnp.float32)
     packed = jnp.einsum(
         "rbk,sb->rsk",

time: 116 us -> 112 us (0.966)
  blocking collectives: 44.1 us -> 31.1 us
  waiting for transfers between devices: 0.04 us -> 8.55 us
    psum x1 -> x2, blocking collectives: 44.1 us -> 31.1 us  [body(): column_sq = jax.lax.psum(column_sq, axis_name=pp)]
    reduce_scatter x1, waiting for transfers between devices: 0.02 us -> 8.54 us  [body(): lax.psum_scatter(ordered, 'dp', scatter_dimension=0, tiled=True, axis_ind...]
  transfers between devices with their start and end apart: 1 -> 1, of which waited for: 0 -> 1; matrix products, arithmetic and copies ran while one was open for 11% -> 11% of each run, Pallas kernels for 0% -> 0%
where the time goes in v1:
time: 112 us; the launch traced here: 111 us
  blocking collectives  31.1 us (28%)
  local copies, waits for them, and re-layouts  30.6 us (27%)
  matrix products  16.2 us (14%)
  between operations  14.1 us (13%)
  other arithmetic  10.5 us (9%)
  waiting for transfers between devices  8.55 us (8%)
    psum x2, blocking collectives, body(): column_sq = jax.lax.psum(column_sq, axis_name=pp)  31.1 us
    unnamed x15, local copies, waits for them, and re-layouts  18.9 us
    reshape x1, local copies, waits for them, and re-layouts, body(): local.reshape(local_rows, blocks, 128)  9.3 us
    reduce_scatter x1, waiting for transfers between devices, body(): lax.psum_scatter(ordered, 'dp', scatter_dimension=0, tiled=True, axis_ind...  8.54 us
    dot_general x1, matrix products, body(): lax.dot_general(features, out_grads, (((0,), (0,)), ((), ())), preferred_...  8.02 us
    dot_general x1, matrix products, body(): jnp.einsum('rbk,sb->rsk', local.reshape(local_rows, blocks, 128), picker,...  7.42 us
    broadcast_in_dim x1, other arithmetic, body(): jnp.where(hot_col[None, :], jnp.float32(0.0), local).astype(jnp.bfloat16)  5.88 us
    select_n x1, other arithmetic, body(): new_second = jnp.where(hot_col[None, :], squared, second)  4.64 us
  transfers between devices with their start and end apart: 1, of which 1 were waited for; matrix products, arithmetic and copies ran while one was open for 11% of the time, Pallas kernels for 0%

profile of v1, /device:TPU:0, one launch (start us, length us, event | category | flops | bytes accessed | tf_op | source)
XLA Modules:
  0.0 111.0 jit_solution(15563694525048485234)
XLA Ops:
  7.2 0.0 copy-start
  7.2 0.0 reduce-scatter.2.cloned.1.call-start
  7.2 6.6 %copy.12 = bf16[1,2048,1024]{1,2,0:T(8,128)(2,1)} copy(bf16[1,2048,1024]{2,1,0:T(8,128)(2,1)} %param.9) | data formatting | bytes 8388608 | tf_op args[2]
  13.8 0.0 copy-done
  13.8 8.0 %multiply_reduce_fusion = (f32[1024]{0:T(1024)S(1)}, f32[2048,1024]{0,1:T(8,128)}) fusion(bf16[640,2048]{1,0:T(8,128)(2,1)S(1)} %copy-done, bf16[640,1024]{1,0:T(8,128)(2,1)} %param.8, bf16[1,2048,1024]{1,2,0:T(8,128)(2,1)} %copy.12), kind=kOutput, calls=%fused_computation.2 | convolution fusion | flops 2692742144 | bytes 16519168 | tf_op jit(solution)/shard_map/dot_general | solution.py:16
  21.8 0.0 copy-start.2
  21.8 9.3 %copy.13 = f32[2048,8,128]{2,1,0:T(8,128)} copy(f32[2048,8,128]{0,2,1:T(8,128)} %bitcast.58) | data formatting | bytes 16777216 | tf_op jit(solution)/shard_map/reshape | solution.py:30
  31.1 0.0 copy-done.2
  31.1 7.4 %convolution_bitcast_fusion = f32[2048,4,128]{2,1,0:T(4,128)S(1)} fusion(f32[2048,8,128]{2,1,0:T(8,128)} %copy.13, s32[8]{0:T(128)S(1)} %copy-done.2), kind=kOutput, calls=%fused_computation.4 | convolution fusion | flops 100663328 | bytes 12582944 | tf_op jit(solution)/shard_map/rbk,sb->rsk/dot_general | solution.py:28
  38.6 0.3 fusion.9
  38.8 0.9 bitcast_dynamic-update-slice_fusion.7
  39.7 0.9 bitcast_dynamic-update-slice_fusion.6
  40.6 0.8 bitcast_dynamic-update-slice_fusion.5
  41.5 0.8 bitcast_dynamic-update-slice_fusion.4
  42.3 0.9 bitcast_dynamic-update-slice_fusion.3
  43.1 0.8 bitcast_dynamic-update-slice_fusion.2
  44.0 0.8 bitcast_dynamic-update-slice_fusion.1
  44.8 0.8 bitcast_dynamic-update-slice_fusion
  45.7 0.0 reduce-scatter.2.cloned.1.call-update
  45.7 0.1 broadcast_bitcast_fusion
  45.8 5.9 %fusion = bf16[1,2048,1024]{1,2,0:T(8,128)(2,1)} fusion(f32[2048,1024]{0,1:T(8,128)} %get-tuple-element.22, pred[1024]{0:T(1024)(128)(4,1)S(1)} %broadcast_bitcast_fusion), kind=kLoop, calls=%fused_computation.3 | loop fusion | flops 2097152 | bytes 12583936 | tf_op jit(solution)/shard_map/broadcast_in_dim | solution.py:22
  51.6 6.3 %copy.14 = bf16[1,2048,1024]{2,1,0:T(8,128)(2,1)} copy(bf16[1,2048,1024]{1,2,0:T(8,128)(2,1)} %fusion) | data formatting | bytes 8388608
  57.9 8.6 %psum.14 = f32[1024]{0:T(1024)S(1)} all-reduce(f32[1024]{0:T(1024)S(1)} %get-tuple-element.21), channel_id=1, replica_groups=mesh['dp'=8,'rep'=4] {'rep'}, use_global_device_ids=true, to_apply=%region_2.3 | all-reduce | flops 1024 | bytes 8192 | tf_op jit(solution)/shard_map/psum | solution.py:26
  66.5 22.5 %psum.15 = f32[1024]{0:T(1024)S(1)} all-reduce(f32[1024]{0:T(1024)S(1)} %psum.14), channel_id=1, replica_groups=mesh['dp'=8,'rep'=4] {'dp'}, use_global_device_ids=true, to_apply=%region_3.4 | all-reduce | flops 1024 | bytes 8192 | tf_op jit(solution)/shard_map/psum | solution.py:26
  89.0 0.0 copy-start.1
  89.1 8.5 %reduce-scatter.2.cloned.1.call-done = f32[256,512]{1,0:T(8,128)} async-done(((f32[2048,512]{1,0:T(8,128)}), f32[256,512]{1,0:T(8,128)}) %reduce-scatter.2.cloned.1.call-update) | async-done | bytes 524304 | tf_op jit(solution)/shard_map/reduce_scatter | solution.py:37
  97.6 1.2 %reshape.42 = f32[256,4,128]{2,1,0:T(4,128)S(1)} reshape(f32[256,512]{1,0:T(8,128)} %reduce-scatter.2.cloned.1.call-done) | data formatting | bytes 1048576 | tf_op jit(solution)/shard_map/reshape | solution.py:43
  98.8 0.7 fusion.4
  99.5 4.6 %fusion.2 = (f32[256,1024]{1,0:T(8,128)}, f32[256,1024]{1,0:T(8,128)}, f32[256,1024]{1,0:T(8,128)}) fusion(f32[256,1024]{1,0:T(8,128)} %param.12, f32[32,8,8,128]{3,2,1,0:T(8,128)S(1)} %bitcast.59, f32[1024]{0:T(1024)S(1)} %maximum_divide_fusion, pred[1024]{0:T(1024)(128)(4,1)S(1)} %broadcast_bitcast_fusion, f32[256,1024]{1,0:T(8,128)} %param.10, ...), kind=kLoop, calls=%fused_computation.10 | loop fusion | flops 4456448 | bytes 7345152 | tf_op jit(solution)/shard_map/jit(_where)/select_n | solution.py:57
  104.2 0.0 copy-done.1
  (2 shorter events, 0.0 us)
Async XLA Ops:
  7.2 6.6 %copy-start = (bf16[640,2048]{1,0:T(8,128)(2,1)S(1)}, bf16[640,2048]{1,0:T(8,128)(2,1)}, u32[]{:S(2)}) copy-start(bf16[640,2048]{1,0:T(8,128)(2,1)} %param.7) | copy-start | bytes 7864324
  7.2 90.4 %reduce-scatter.2.cloned.1.call-start = ((), (), s32[]{:S(2)}) async-start(), calls=%async_computation.1 | async-start | bytes 4718592 | tf_op jit(solution)/shard_map/reduce_scatter | solution.py:37
  21.8 9.3 %copy-start.2 = (s32[8]{0:T(128)S(1)}, s32[8]{0:T(128)}, u32[]{:S(2)}) copy-start(s32[8]{0:T(128)} %param.13) | copy-start | bytes 100
  89.0 15.1 %copy-start.1 = (f32[1024]{0:T(1024)}, f32[1024]{0:T(1024)S(1)}, u32[]{:S(2)}) copy-start(f32[1024]{0:T(1024)S(1)} %psum.15) | copy-start | bytes 12292
Sparse Core Ops, SparseCore 0:
  45.8 51.7 reduce-scatter.1
